TPU v7x, 32 devices: a whole 2x2x4 slice. The times are simulated.
32 devices in a mesh: level: 2 (over core), gx: 4 (over y, x), yz: 4 (over z).
Axes of the slice: x: 2, y: 2, z: 4, core: 2. Of those that a mesh axis runs over, the one named last changes fastest.
Arguments:
- init_field: float32 [128, 64, 256], P('gx', 'yz'), may hold values from -6 to 6
- source: float32 [128, 64, 256], P('gx', 'yz'), may hold values from -4 to 4
- damping: float32 [128, 64, 256], P('gx', 'yz'), may hold values from 0.05 to 2
Outputs:
- final_states: float32 [2, 128, 64, 256], P('level', 'gx', 'yz')
All inputs are finite; a program needn't handle non-finite values.
Results may differ from a plain program's by a relative error of at most 0.0001.
Values sent between devices are 32-bit elements; how exact they have to be, the bound alone decides.
A program may use at most 64 MiB of HBM per device.

v0:
```python
import jax
import jax.numpy as jnp
from jax import lax
from jax.sharding import PartitionSpec as P

STEPS = 3
ITERS = 3


diffusion_number = 1.0


def extended(cells, sides, width):
    for axis, dim in sides:
        count = lax.axis_size(axis)
        ends = count - 1
        head = lax.slice_in_dim(cells, 0, width, axis=dim)
        tail = lax.slice_in_dim(cells, cells.shape[dim] - width, cells.shape[dim], axis=dim)
        cells = jnp.concatenate(
            [
                lax.ppermute(tail, axis, [(i, (i + 1) % count) for i in range(ends)]),
                cells,
                lax.ppermute(head, axis, [((i + 1) % count, i) for i in range(ends)]),
            ],
            axis=dim,
        )
    return cells


def passed_along(block, axis, distance):
    devices = range(lax.axis_size(axis))
    route = [(i - distance, i) for i in devices if i - distance in devices]
    return lax.ppermute(block, axis, route)


def stencil_from(padded, field, damping):
    beside = padded[2:, 1:-1, :] + padded[:-2, 1:-1, :]
    beside = beside + padded[1:-1, 2:, :] + padded[1:-1, :-2, :]
    zero_plane = jnp.zeros_like(field[:, :, :1])
    beside = beside + jnp.concatenate([field[:, :, 1:], zero_plane], axis=2)
    beside = beside + jnp.concatenate([zero_plane, field[:, :, :-1]], axis=2)
    return damping * field + diffusion_number * (6.0 * field - beside)


def operate(field, damping):
    padded = extended(field, (("gx", 0), ("yz", 1)), 1)
    return field + stencil_from(padded, field, damping)


def two_products(resid, image):
    return lax.psum((jnp.sum(resid * resid), jnp.sum(resid * image)), ("gx", "yz"))


def solve(target, guess, damping):
    answer = guess
    resid = target - operate(answer, damping)
    image = operate(resid, damping)
    norm_now, product = two_products(resid, image)
    alpha = norm_now / product
    direction, along = (resid, image)
    for step in range(ITERS):
        answer = answer + alpha * direction
        resid = resid - alpha * along
        if step + 1 < ITERS:
            image = operate(resid, damping)
            norm_next, product = two_products(resid, image)
            ratio = norm_next / norm_now
            alpha = norm_next / (product - ratio * norm_next / alpha)
            direction = resid + ratio * direction
            along = image + ratio * along
            norm_now = norm_next
    return answer


def per_device(init_field, source, damping):
    upper = lax.axis_index("level") == 1
    state = init_field
    older = jnp.where(upper, init_field, jnp.zeros_like(init_field))
    for rounds in range(STEPS + 1):
        if rounds == 0:
            extra = jnp.zeros_like(init_field)
        else:
            incoming = passed_along(state, "level", 1)
            change = incoming - older
            older = incoming
            padded = extended(change, (("gx", 0), ("yz", 1)), 1)
            extra = 0.5 * stencil_from(padded, change, damping)
        fresh = solve(state + source + extra, state, damping)
        if rounds == 0:
            state = jnp.where(upper, state, fresh)
        elif rounds == STEPS:
            state = jnp.where(upper, fresh, state)
        else:
            state = fresh
    return state[None]


def solution(mesh):
    in_specs = (P("gx", "yz", None), P("gx", "yz", None), P("gx", "yz", None))
    out_specs = P("level", "gx", "yz", None)
    return jax.shard_map(
        per_device, mesh=mesh, in_specs=in_specs, out_specs=out_specs, check_vma=False
    )
```

profile of v0, /device:TPU:0, one launch (start us, length us, event | category | flops | bytes accessed | tf_op | source)
XLA Modules:
  0.0 858.0 jit_solution(10552199963659555347)
XLA Ops:
  0.7 4.9 collective-permute-start.1
  12.6 4.7 collective-permute-start.3
  30.7 4.9 collective-permute-start.7
  38.3 40.1 %all-reduce.49 = (f32[]{:T(128)}, f32[]{:T(128)}) all-reduce(f32[]{:T(128)} %get-tuple-element.28, f32[]{:T(128)} %get-tuple-element.27), channel_id=1, replica_groups=mesh['level'=2,'gx'=4,'yz'=4] {'gx','yz'}, use_global_device_ids=true, to_apply=%region_1.2 | all-reduce | flops 2 | bytes 16 | tf_op jit(solution)/shard_map/psum | solution.py:51
  83.3 8.2 collective-permute-done.8
  92.8 4.5 collective-permute-start.11
  100.9 39.7 %all-reduce.48 = (f32[]{:T(128)}, f32[]{:T(128)}) all-reduce(f32[]{:T(128)} %get-tuple-element.26, f32[]{:T(128)} %get-tuple-element.25), channel_id=1, replica_groups=mesh['level'=2,'gx'=4,'yz'=4] {'gx','yz'}, use_global_device_ids=true, to_apply=%region_5.6 | all-reduce | flops 2 | bytes 16 | tf_op jit(solution)/shard_map/psum | solution.py:51
  149.0 5.5 collective-permute-done.12
  155.9 4.5 collective-permute-start.15
  163.2 39.7 %all-reduce.47 = (f32[]{:T(128)}, f32[]{:T(128)}) all-reduce(f32[]{:T(128)} %get-tuple-element.24, f32[]{:T(128)} %get-tuple-element.23), channel_id=1, replica_groups=mesh['level'=2,'gx'=4,'yz'=4] {'gx','yz'}, use_global_device_ids=true, to_apply=%region_9.10 | all-reduce | flops 2 | bytes 16 | tf_op jit(solution)/shard_map/psum | solution.py:51
  212.1 7.1 collective-permute-start.18
  221.8 4.5 collective-permute-start.24
  227.8 4.7 collective-permute-start.20
  234.9 5.4 collective-permute-start.26
  241.8 5.1 collective-permute-done.25
  248.2 4.9 collective-permute-start.28
  255.8 39.8 %all-reduce.46 = (f32[]{:T(128)}, f32[]{:T(128)}) all-reduce(f32[]{:T(128)} %get-tuple-element.22, f32[]{:T(128)} %get-tuple-element.21), channel_id=1, replica_groups=mesh['level'=2,'gx'=4,'yz'=4] {'gx','yz'}, use_global_device_ids=true, to_apply=%region_13.14 | all-reduce | flops 2 | bytes 16 | tf_op jit(solution)/shard_map/psum | solution.py:51
  299.6 8.9 %collective-permute-done.29 = f32[1,16,256]{2,1,0:T(8,128)S(1)} collective-permute-done((f32[1,16,256]{2,1,0:T(8,128)S(1)}, f32[1,16,256]{2,1,0:T(8,128)S(1)}, u32[]{:S(2)}, u32[]{:S(2)}) %collective-permute-start.29) | collective-permute-done | bytes 16416 | tf_op jit(solution)/shard_map/ppermute | solution.py:23
  309.9 4.5 collective-permute-start.32
  317.9 39.7 %all-reduce.45 = (f32[]{:T(128)}, f32[]{:T(128)}) all-reduce(f32[]{:T(128)} %get-tuple-element.20, f32[]{:T(128)} %get-tuple-element.19), channel_id=1, replica_groups=mesh['level'=2,'gx'=4,'yz'=4] {'gx','yz'}, use_global_device_ids=true, to_apply=%region_17.18 | all-reduce | flops 2 | bytes 16 | tf_op jit(solution)/shard_map/psum | solution.py:51
  366.0 5.5 collective-permute-done.33
  372.8 4.5 collective-permute-start.36
  380.0 39.7 %all-reduce.44 = (f32[]{:T(128)}, f32[]{:T(128)}) all-reduce(f32[]{:T(128)} %get-tuple-element.18, f32[]{:T(128)} %get-tuple-element.17), channel_id=1, replica_groups=mesh['level'=2,'gx'=4,'yz'=4] {'gx','yz'}, use_global_device_ids=true, to_apply=%region_21.22 | all-reduce | flops 2 | bytes 16 | tf_op jit(solution)/shard_map/psum | solution.py:51
  428.8 7.2 collective-permute-start.39
  438.6 4.5 collective-permute-start.45
  444.6 4.9 collective-permute-start.41
  451.7 5.4 collective-permute-start.47
  458.5 5.1 collective-permute-done.46
  465.0 4.9 collective-permute-start.49
  472.6 39.8 %all-reduce.43 = (f32[]{:T(128)}, f32[]{:T(128)}) all-reduce(f32[]{:T(128)} %get-tuple-element.16, f32[]{:T(128)} %get-tuple-element.15), channel_id=1, replica_groups=mesh['level'=2,'gx'=4,'yz'=4] {'gx','yz'}, use_global_device_ids=true, to_apply=%region_25.26 | all-reduce | flops 2 | bytes 16 | tf_op jit(solution)/shard_map/psum | solution.py:51
  516.4 8.9 %collective-permute-done.50 = f32[1,16,256]{2,1,0:T(8,128)S(1)} collective-permute-done((f32[1,16,256]{2,1,0:T(8,128)S(1)}, f32[1,16,256]{2,1,0:T(8,128)S(1)}, u32[]{:S(2)}, u32[]{:S(2)}) %collective-permute-start.50) | collective-permute-done | bytes 16416 | tf_op jit(solution)/shard_map/ppermute | solution.py:23
  526.7 4.5 collective-permute-start.53
  534.7 39.8 %all-reduce.42 = (f32[]{:T(128)}, f32[]{:T(128)}) all-reduce(f32[]{:T(128)} %get-tuple-element.14, f32[]{:T(128)} %get-tuple-element.13), channel_id=1, replica_groups=mesh['level'=2,'gx'=4,'yz'=4] {'gx','yz'}, use_global_device_ids=true, to_apply=%region_29.30 | all-reduce | flops 2 | bytes 16 | tf_op jit(solution)/shard_map/psum | solution.py:51
  582.8 5.4 collective-permute-done.54
  589.6 4.5 collective-permute-start.57
  596.9 39.7 %all-reduce.41 = (f32[]{:T(128)}, f32[]{:T(128)}) all-reduce(f32[]{:T(128)} %get-tuple-element.12, f32[]{:T(128)} %get-tuple-element.11), channel_id=1, replica_groups=mesh['level'=2,'gx'=4,'yz'=4] {'gx','yz'}, use_global_device_ids=true, to_apply=%region_33.34 | all-reduce | flops 2 | bytes 16 | tf_op jit(solution)/shard_map/psum | solution.py:51
  644.9 7.2 collective-permute-start.60
  654.7 4.5 collective-permute-start.66
  660.7 4.7 collective-permute-start.62
  667.8 5.4 collective-permute-start.68
  674.7 5.1 collective-permute-done.67
  681.1 4.9 collective-permute-start.70
  688.6 39.8 %all-reduce.40 = (f32[]{:T(128)}, f32[]{:T(128)}) all-reduce(f32[]{:T(128)} %get-tuple-element.10, f32[]{:T(128)} %get-tuple-element.9), channel_id=1, replica_groups=mesh['level'=2,'gx'=4,'yz'=4] {'gx','yz'}, use_global_device_ids=true, to_apply=%region_37.38 | all-reduce | flops 2 | bytes 16 | tf_op jit(solution)/shard_map/psum | solution.py:51
  732.7 8.9 %collective-permute-done.71 = f32[1,16,256]{2,1,0:T(8,128)S(1)} collective-permute-done((f32[1,16,256]{2,1,0:T(8,128)S(1)}, f32[1,16,256]{2,1,0:T(8,128)S(1)}, u32[]{:S(2)}, u32[]{:S(2)}) %collective-permute-start.71) | collective-permute-done | bytes 16416 | tf_op jit(solution)/shard_map/ppermute | solution.py:23
  743.0 4.5 collective-permute-start.74
  751.0 39.7 %all-reduce.39 = (f32[]{:T(128)}, f32[]{:T(128)}) all-reduce(f32[]{:T(128)} %get-tuple-element.8, f32[]{:T(128)} %get-tuple-element.7), channel_id=1, replica_groups=mesh['level'=2,'gx'=4,'yz'=4] {'gx','yz'}, use_global_device_ids=true, to_apply=%region_41.42 | all-reduce | flops 2 | bytes 16 | tf_op jit(solution)/shard_map/psum | solution.py:51
  799.2 5.5 collective-permute-done.75
  813.3 39.7 %all-reduce.38 = (f32[]{:T(128)}, f32[]{:T(128)}) all-reduce(f32[]{:T(128)} %get-tuple-element.6, f32[]{:T(128)} %get-tuple-element.5), channel_id=1, replica_groups=mesh['level'=2,'gx'=4,'yz'=4] {'gx','yz'}, use_global_device_ids=true, to_apply=%region_45.46 | all-reduce | flops 2 | bytes 16 | tf_op jit(solution)/shard_map/psum | solution.py:51
  (233 shorter events, 142.6 us)
Async XLA Ops:
  0.7 6.3 collective-permute-start.1
  12.6 6.3 collective-permute-start.3
  29.4 6.4 collective-permute-start.6
  30.7 6.5 collective-permute-start.7
  81.9 9.6 %collective-permute-start.8 = (f32[1,16,256]{2,1,0:T(8,128)S(1)}, f32[1,16,256]{2,1,0:T(8,128)S(1)}, u32[]{:S(2)}, u32[]{:S(2)}) collective-permute-start(f32[1,16,256]{2,1,0:T(8,128)S(1)} %get-tuple-element.164), channel_id=1, source_target_pairs={{4,0},{8,4},{12,8},{5,1},{9,5},{13,9},{6,2},{10,6},{14,10},{7,3},{... | collective-permute-start | bytes 49160 | tf_op jit(solution)/shard_map/ppermute | solution.py:23
  147.6 7.0 collective-permute-start.12
  208.4 12.0 %collective-permute-start.22 = (f32[1,16,256]{2,1,0:T(8,128)S(1)}, f32[1,16,256]{2,1,0:T(8,128)S(1)}, u32[]{:S(2)}, u32[]{:S(2)}) collective-permute-start(f32[1,16,256]{2,1,0:T(8,128)S(1)} %get-tuple-element.157), channel_id=1, source_target_pairs={{0,4},{4,8},{8,12},{1,5},{5,9},{9,13},{2,6},{6,10},{10,14},{3,7},{... | collective-permute-start | bytes 49160 | tf_op jit(solution)/shard_map/ppermute | solution.py:21
  209.7 10.7 %collective-permute-start.21 = (f32[1,16,256]{2,1,0:T(8,128)S(1)}, f32[1,16,256]{2,1,0:T(8,128)S(1)}, u32[]{:S(2)}, u32[]{:S(2)}) collective-permute-start(f32[1,16,256]{2,1,0:T(8,128)S(1)} %get-tuple-element.158), channel_id=1, source_target_pairs={{4,0},{8,4},{12,8},{5,1},{9,5},{13,9},{6,2},{10,6},{14,10},{7,3},{... | collective-permute-start | bytes 49160 | tf_op jit(solution)/shard_map/ppermute | solution.py:23
  212.1 14.3 %collective-permute-start.18 = (f32[1,16,256]{2,1,0:T(8,128)S(1)}, f32[1,16,256]{2,1,0:T(8,128)S(1)}, u32[]{:S(2)}, u32[]{:S(2)}) collective-permute-start(f32[1,16,256]{2,1,0:T(8,128)S(1)} %get-tuple-element.155), channel_id=1, source_target_pairs={{0,4},{4,8},{8,12},{1,5},{5,9},{9,13},{2,6},{6,10},{10,14},{3,7},{... | collective-permute-start | bytes 49160 | tf_op jit(solution)/shard_map/ppermute | solution.py:21
  219.2 7.2 collective-permute-start.17
  220.5 12.2 %collective-permute-start.23 = (f32[34,1,256]{2,1,0:T(1,128)S(1)}, f32[34,1,256]{2,1,0:T(1,128)S(1)}, u32[]{:S(2)}, u32[]{:S(2)}) collective-permute-start(f32[34,1,256]{2,1,0:T(1,128)S(1)} %get-tuple-element.89), channel_id=1, source_target_pairs={{1,0},{2,1},{3,2},{5,4},{6,5},{7,6},{9,8},{10,9},{11,10},{13,12},{... | collective-permute-start | bytes 104456 | tf_op jit(solution)/shard_map/ppermute | solution.py:23
  221.8 10.9 %collective-permute-start.24 = (f32[34,1,256]{2,1,0:T(1,128)S(1)}, f32[34,1,256]{2,1,0:T(1,128)S(1)}, u32[]{:S(2)}, u32[]{:S(2)}) collective-permute-start(f32[34,1,256]{2,1,0:T(1,128)S(1)} %get-tuple-element.90), channel_id=1, source_target_pairs={{0,1},{1,2},{2,3},{4,5},{5,6},{6,7},{8,9},{9,10},{10,11},{12,13},{... | collective-permute-start | bytes 104456 | tf_op jit(solution)/shard_map/ppermute | solution.py:21
  226.5 6.2 collective-permute-start.19
  227.8 6.3 collective-permute-start.20
  234.9 6.9 collective-permute-start.26
  240.3 6.5 collective-permute-start.25
  246.9 6.4 collective-permute-start.27
  248.2 6.5 collective-permute-start.28
  298.2 10.3 %collective-permute-start.29 = (f32[1,16,256]{2,1,0:T(8,128)S(1)}, f32[1,16,256]{2,1,0:T(8,128)S(1)}, u32[]{:S(2)}, u32[]{:S(2)}) collective-permute-start(f32[1,16,256]{2,1,0:T(8,128)S(1)} %get-tuple-element.144), channel_id=1, source_target_pairs={{4,0},{8,4},{12,8},{5,1},{9,5},{13,9},{6,2},{10,6},{14,10},{7,3},{... | collective-permute-start | bytes 49160 | tf_op jit(solution)/shard_map/ppermute | solution.py:23
  364.5 6.9 collective-permute-start.33
  425.0 12.3 %collective-permute-start.43 = (f32[1,16,256]{2,1,0:T(8,128)S(1)}, f32[1,16,256]{2,1,0:T(8,128)S(1)}, u32[]{:S(2)}, u32[]{:S(2)}) collective-permute-start(f32[1,16,256]{2,1,0:T(8,128)S(1)} %get-tuple-element.137), channel_id=1, source_target_pairs={{0,4},{4,8},{8,12},{1,5},{5,9},{9,13},{2,6},{6,10},{10,14},{3,7},{... | collective-permute-start | bytes 49160 | tf_op jit(solution)/shard_map/ppermute | solution.py:21
  426.3 11.0 %collective-permute-start.42 = (f32[1,16,256]{2,1,0:T(8,128)S(1)}, f32[1,16,256]{2,1,0:T(8,128)S(1)}, u32[]{:S(2)}, u32[]{:S(2)}) collective-permute-start(f32[1,16,256]{2,1,0:T(8,128)S(1)} %get-tuple-element.138), channel_id=1, source_target_pairs={{4,0},{8,4},{12,8},{5,1},{9,5},{13,9},{6,2},{10,6},{14,10},{7,3},{... | collective-permute-start | bytes 49160 | tf_op jit(solution)/shard_map/ppermute | solution.py:23
  428.8 14.4 %collective-permute-start.39 = (f32[1,16,256]{2,1,0:T(8,128)S(1)}, f32[1,16,256]{2,1,0:T(8,128)S(1)}, u32[]{:S(2)}, u32[]{:S(2)}) collective-permute-start(f32[1,16,256]{2,1,0:T(8,128)S(1)} %get-tuple-element.135), channel_id=1, source_target_pairs={{0,4},{4,8},{8,12},{1,5},{5,9},{9,13},{2,6},{6,10},{10,14},{3,7},{... | collective-permute-start | bytes 49160 | tf_op jit(solution)/shard_map/ppermute | solution.py:21
  435.9 7.2 collective-permute-start.38
  437.3 12.3 %collective-permute-start.44 = (f32[34,1,256]{2,1,0:T(1,128)S(1)}, f32[34,1,256]{2,1,0:T(1,128)S(1)}, u32[]{:S(2)}, u32[]{:S(2)}) collective-permute-start(f32[34,1,256]{2,1,0:T(1,128)S(1)} %get-tuple-element.79), channel_id=1, source_target_pairs={{1,0},{2,1},{3,2},{5,4},{6,5},{7,6},{9,8},{10,9},{11,10},{13,12},{... | collective-permute-start | bytes 104456 | tf_op jit(solution)/shard_map/ppermute | solution.py:23
  438.6 11.0 %collective-permute-start.45 = (f32[34,1,256]{2,1,0:T(1,128)S(1)}, f32[34,1,256]{2,1,0:T(1,128)S(1)}, u32[]{:S(2)}, u32[]{:S(2)}) collective-permute-start(f32[34,1,256]{2,1,0:T(1,128)S(1)} %get-tuple-element.80), channel_id=1, source_target_pairs={{0,1},{1,2},{2,3},{4,5},{5,6},{6,7},{8,9},{9,10},{10,11},{12,13},{... | collective-permute-start | bytes 104456 | tf_op jit(solution)/shard_map/ppermute | solution.py:21
  443.3 6.4 collective-permute-start.40
  444.6 6.3 collective-permute-start.41
  451.7 6.9 collective-permute-start.47
  457.1 6.5 collective-permute-start.46
  463.7 6.4 collective-permute-start.48
  465.0 6.5 collective-permute-start.49
  515.0 10.4 %collective-permute-start.50 = (f32[1,16,256]{2,1,0:T(8,128)S(1)}, f32[1,16,256]{2,1,0:T(8,128)S(1)}, u32[]{:S(2)}, u32[]{:S(2)}) collective-permute-start(f32[1,16,256]{2,1,0:T(8,128)S(1)} %get-tuple-element.124), channel_id=1, source_target_pairs={{4,0},{8,4},{12,8},{5,1},{9,5},{13,9},{6,2},{10,6},{14,10},{7,3},{... | collective-permute-start | bytes 49160 | tf_op jit(solution)/shard_map/ppermute | solution.py:23
  581.4 6.9 collective-permute-start.54
  641.8 11.6 %collective-permute-start.64 = (f32[1,16,256]{2,1,0:T(8,128)S(1)}, f32[1,16,256]{2,1,0:T(8,128)S(1)}, u32[]{:S(2)}, u32[]{:S(2)}) collective-permute-start(f32[1,16,256]{2,1,0:T(8,128)S(1)} %get-tuple-element.117), channel_id=1, source_target_pairs={{0,4},{4,8},{8,12},{1,5},{5,9},{9,13},{2,6},{6,10},{10,14},{3,7},{... | collective-permute-start | bytes 49160 | tf_op jit(solution)/shard_map/ppermute | solution.py:21
  643.1 10.3 %collective-permute-start.63 = (f32[1,16,256]{2,1,0:T(8,128)S(1)}, f32[1,16,256]{2,1,0:T(8,128)S(1)}, u32[]{:S(2)}, u32[]{:S(2)}) collective-permute-start(f32[1,16,256]{2,1,0:T(8,128)S(1)} %get-tuple-element.118), channel_id=1, source_target_pairs={{4,0},{8,4},{12,8},{5,1},{9,5},{13,9},{6,2},{10,6},{14,10},{7,3},{... | collective-permute-start | bytes 49160 | tf_op jit(solution)/shard_map/ppermute | solution.py:23
  644.9 14.4 %collective-permute-start.60 = (f32[1,16,256]{2,1,0:T(8,128)S(1)}, f32[1,16,256]{2,1,0:T(8,128)S(1)}, u32[]{:S(2)}, u32[]{:S(2)}) collective-permute-start(f32[1,16,256]{2,1,0:T(8,128)S(1)} %get-tuple-element.115), channel_id=1, source_target_pairs={{0,4},{4,8},{8,12},{1,5},{5,9},{9,13},{2,6},{6,10},{10,14},{3,7},{... | collective-permute-start | bytes 49160 | tf_op jit(solution)/shard_map/ppermute | solution.py:21
  652.1 7.2 collective-permute-start.59
  653.4 12.2 %collective-permute-start.65 = (f32[34,1,256]{2,1,0:T(1,128)S(1)}, f32[34,1,256]{2,1,0:T(1,128)S(1)}, u32[]{:S(2)}, u32[]{:S(2)}) collective-permute-start(f32[34,1,256]{2,1,0:T(1,128)S(1)} %get-tuple-element.69), channel_id=1, source_target_pairs={{1,0},{2,1},{3,2},{5,4},{6,5},{7,6},{9,8},{10,9},{11,10},{13,12},{... | collective-permute-start | bytes 104456 | tf_op jit(solution)/shard_map/ppermute | solution.py:23
  654.7 10.9 %collective-permute-start.66 = (f32[34,1,256]{2,1,0:T(1,128)S(1)}, f32[34,1,256]{2,1,0:T(1,128)S(1)}, u32[]{:S(2)}, u32[]{:S(2)}) collective-permute-start(f32[34,1,256]{2,1,0:T(1,128)S(1)} %get-tuple-element.70), channel_id=1, source_target_pairs={{0,1},{1,2},{2,3},{4,5},{5,6},{6,7},{8,9},{9,10},{10,11},{12,13},{... | collective-permute-start | bytes 104456 | tf_op jit(solution)/shard_map/ppermute | solution.py:21
  659.4 6.2 collective-permute-start.61
  660.7 6.3 collective-permute-start.62
  667.8 6.9 collective-permute-start.68
  673.2 6.5 collective-permute-start.67
  679.8 6.4 collective-permute-start.69
  681.1 6.5 collective-permute-start.70
  731.3 10.4 %collective-permute-start.71 = (f32[1,16,256]{2,1,0:T(8,128)S(1)}, f32[1,16,256]{2,1,0:T(8,128)S(1)}, u32[]{:S(2)}, u32[]{:S(2)}) collective-permute-start(f32[1,16,256]{2,1,0:T(8,128)S(1)} %get-tuple-element.104), channel_id=1, source_target_pairs={{4,0},{8,4},{12,8},{5,1},{9,5},{13,9},{6,2},{10,6},{14,10},{7,3},{... | collective-permute-start | bytes 49160 | tf_op jit(solution)/shard_map/ppermute | solution.py:23
  797.7 6.9 collective-permute-start.75
  (41 other events, 203.0 us)
where the time goes:
time: 861 us; the launch traced here: 858 us
  blocking collectives  477 us (55%)
  starting transfers between devices  204 us (24%)
  waiting for transfers between devices  103 us (12%)
  between operations  39.6 us (5%)
  other arithmetic  27.4 us (3%)
    psum x12, blocking collectives, two_products(): lax.psum((jnp.sum(resid * resid), jnp.sum(resid * image)), ('gx', 'yz'))  477 us
    ppermute x38, starting transfers between devices, extended(): lax.ppermute(tail, axis, [(i, (i + 1) % count) for i in range(ends)])  150 us
    ppermute x38, waiting for transfers between devices, extended(): lax.ppermute(head, axis, [((i + 1) % count, i) for i in range(ends)])  79.6 us
    ppermute x38, starting transfers between devices, extended(): lax.ppermute(head, axis, [((i + 1) % count, i) for i in range(ends)])  49.4 us
    ppermute x38, waiting for transfers between devices, extended(): lax.ppermute(tail, axis, [(i, (i + 1) % count) for i in range(ends)])  23.4 us
  transfers between devices with their start and end apart: 79, of which 42 were waited for; matrix products, arithmetic and copies ran while one was open for 1% of the time, Pallas kernels for 0%

commit v1 on v0

v1 whole, which is shorter than its diff:
```python
import functools

import jax
import jax.numpy as jnp
from jax import lax
from jax.experimental import pallas as pl
from jax.experimental.pallas import tpu as pltpu
from jax.sharding import PartitionSpec as P

STEPS = 3
ITERS = 3
PX = 3
PY = 8
LANES = 128
MID = 8.025
HALF = 6.975
MESH = pl.DeviceIdType.MESH
DIRS = ((-1, 0), (1, 0), (0, -1), (0, 1), (-1, -1), (-1, 1), (1, -1), (1, 1))


def times_a(c):
    out = [MID * v for v in c] + [jnp.zeros_like(c[0])]
    for k, v in enumerate(c):
        if k == 0:
            out[1] = out[1] + HALF * v
        else:
            out[k + 1] = out[k + 1] + (0.5 * HALF) * v
            out[k - 1] = out[k - 1] + (0.5 * HALF) * v
    return out


def plus(a, b):
    short, long = (a, b) if len(a) < len(b) else (b, a)
    return [x + y for x, y in zip(short, long)] + long[len(short):]


def scaled(s, a):
    return [s * x for x in a]


def cg_coefficients(dots):
    m = [dots[0], dots[1], 2.0 * dots[2] - dots[0], 2.0 * dots[3] - dots[1],
         2.0 * dots[4] - dots[0], 2.0 * dots[5] - dots[1]]

    def inner(a, b):
        total = None
        for i, x in enumerate(a):
            for j, y in enumerate(b):
                term = (x * y) * (0.5 * (m[i + j] + m[abs(i - j)]))
                total = term if total is None else total + term
        return total

    one = jnp.ones_like(m[0])
    resid = [one]
    direction = resid
    image = times_a(resid)
    along = image
    norm_now = m[0]
    alpha = norm_now / inner(resid, image)
    answer = None
    for step in range(ITERS):
        move = scaled(alpha, direction)
        answer = move if answer is None else plus(answer, move)
        if step + 1 < ITERS:
            resid = plus(resid, scaled(-alpha, along))
            image = times_a(resid)
            norm_next = inner(resid, resid)
            product = inner(resid, image)
            ratio = norm_next / norm_now
            alpha = norm_next / (product - ratio * norm_next / alpha)
            direction = plus(resid, scaled(ratio, direction))
            along = plus(image, scaled(ratio, along))
            norm_now = norm_next
    change = plus(times_a(answer), scaled(-1.0, answer))
    return answer, change


def body(sizes, stages, init_ref, source_ref, damp_ref, out_ref, p0, src, dmp, heads_p, heads_c,
         work_p, work_c, base, sums, result, slots, in_sem, send_sem, recv_sem, red_send, red_recv, out_sem):
    levels, nx, ny = sizes
    half = src.shape[0]
    parts = src.shape[1]
    rows = src.shape[2]
    level, gx, yz = lax.axis_index("level"), lax.axis_index("gx"), lax.axis_index("yz")
    xpos = gx * levels + level
    xcount = nx * levels
    x_in = (xpos > 0, xpos < xcount - 1)
    y_in = (yz > 0, yz < ny - 1)

    def exists(dx, dy):
        ok = None
        for d, pair in ((dx, x_in), (dy, y_in)):
            if d != 0:
                c = pair[0] if d < 0 else pair[1]
                ok = c if ok is None else jnp.logical_and(ok, c)
        return ok

    mine = pl.ds(level * half, half)
    loads = []
    for i, (ref, buf, pad) in enumerate(((init_ref, p0, True), (damp_ref, dmp, True), (source_ref, src, False))):
        for z in range(parts):
            lanes = slice(z * LANES, (z + 1) * LANES)
            dst = buf.at[PX:PX + half, z, PY:PY + rows, :] if pad else buf.at[:, z, :, :]
            copy = pltpu.make_async_copy(ref.at[mine, :, lanes], dst, in_sem.at[i, z])
            copy.start()
            loads.append(copy)

    zero_x = jnp.zeros((PX,) + tuple(p0.shape[1:]), jnp.float32)
    zero_y = jnp.zeros((p0.shape[0], parts, PY, LANES), jnp.float32)
    for buf in [p0] + [h.at[n] for h in (heads_p, heads_c) for n in range(STEPS)]:
        @pl.when(jnp.logical_not(x_in[0]))
        def _(buf=buf):
            buf[0:PX] = zero_x

        @pl.when(jnp.logical_not(x_in[1]))
        def _(buf=buf):
            buf[PX + half:] = zero_x

        @pl.when(jnp.logical_not(y_in[0]))
        def _(buf=buf):
            buf[:, :, 0:PY, :] = zero_y

        @pl.when(jnp.logical_not(y_in[1]))
        def _(buf=buf):
            buf[:, :, PY + rows:, :] = zero_y

    def halo_copy(buf, width, slot, k):
        dx, dy = DIRS[k]
        w = width if 0 in (dx, dy) else width - 1
        if w == 0:
            return None

        def spans(d, pad, size):
            if d == 0:
                return slice(pad, pad + size), slice(pad, pad + size)
            if d < 0:
                return slice(pad, pad + w), slice(pad + size, pad + size + w)
            return slice(pad + size - w, pad + size), slice(pad - w, pad)

        sx, tx = spans(dx, PX, half)
        sy, ty = spans(dy, PY, rows)
        to = xpos + dx
        return pltpu.make_async_remote_copy(
            src_ref=buf.at[sx, :, sy, :], dst_ref=buf.at[tx, :, ty, :],
            send_sem=send_sem.at[slot, k], recv_sem=recv_sem.at[slot, k],
            device_id={"level": lax.rem(to + levels, levels), "gx": lax.div(to + levels, levels) - 1, "yz": yz + dy},
            device_id_type=MESH,
        )

    order = (4, 5, 6, 7, 2, 3, 0, 1)

    def send_halo(buf, width, slot):
        for k in order:
            copy = halo_copy(buf, width, slot, k)
            if copy is not None:
                pl.when(exists(*DIRS[k]))(lambda copy=copy: copy.start())

    def wait_halo(buf, width, slot):
        for k in order:
            copy = halo_copy(buf, width, slot, k)
            if copy is not None:
                dx, dy = DIRS[k]
                pl.when(exists(-dx, -dy))(lambda copy=copy: copy.wait_recv())

    def end_halo(buf, width, slot):
        for k in order:
            copy = halo_copy(buf, width, slot, k)
            if copy is not None:
                pl.when(exists(*DIRS[k]))(lambda copy=copy: copy.wait_send())

    def stencil(v, x, start, count):
        lane = lax.broadcasted_iota(jnp.int32, (count, LANES), 1)
        own = pl.ds(start, count)
        centre = [v[x, z, own, :] for z in range(parts)]
        fore = [pltpu.roll(c, 1, 1) for c in centre]
        back = [pltpu.roll(c, LANES - 1, 1) for c in centre]
        out = []
        for z in range(parts):
            near = jnp.where(lane == 0, fore[z - 1] if z > 0 else 0.0, fore[z])
            far = jnp.where(lane == LANES - 1, back[z + 1] if z + 1 < parts else 0.0, back[z])
            beside = v[x - 1, z, own, :] + v[x + 1, z, own, :]
            beside = beside + v[x, z, pl.ds(start - 1, count), :] + v[x, z, pl.ds(start + 1, count), :]
            beside = beside + (near + far)
            out.append((dmp[x, z, own, :] + (7.0 - MID)) * centre[z] - beside)
        return out, centre

    low = jnp.where(y_in[0], 0, PY)
    high = jnp.where(y_in[1], 2 * PY + rows, PY + rows)
    first = jnp.where(x_in[0], 0, PX)
    last = jnp.where(x_in[1], 2 * PX + half, PX + half)

    def fold(block):
        return jnp.sum(block.reshape(-1, 8, LANES), axis=0)

    def powers(head, work):
        zero = jnp.zeros((8, LANES), jnp.float32)
        own = pl.ds(PY, rows)
        totals = []
        for k in range(1, ITERS + 1):
            h = ITERS - k
            start = PY - h
            count = -(-(rows + 2 * h) // 8) * 8
            prev = head if k == 1 else work.at[k - 2]
            row = lax.broadcasted_iota(jnp.int32, (count, LANES), 0) + start

            def plane(x, carry, k=k, h=h, start=start, count=count, prev=prev, row=row):
                t, centre = stencil(prev, x, start, count)
                if h > 0:
                    top = jnp.where(jnp.logical_and(x >= first, x < last), high, 0)
                    ok = jnp.logical_and(row >= low, row < top)
                for z in range(parts):
                    if k == 1:
                        new = t[z] * (1.0 / HALF)
                    else:
                        older = head if k == 2 else work.at[k - 3]
                        new = t[z] * (2.0 / HALF) - older[x, z, pl.ds(start, count), :]
                    if h > 0:
                        new = jnp.where(ok, new, 0.0)
                    work[k - 1, x, z, pl.ds(start, count), :] = new
                return carry

            def inside(x, carry, k=k, prev=prev, plane=plane):
                plane(x, 0)
                a, b = carry
                for z in range(parts):
                    v = prev[x, z, own, :]
                    w = work[k - 1, x, z, own, :]
                    a = a + fold(v * v)
                    b = b + fold(v * w)
                return a, b

            if h > 0:
                lax.fori_loop(PX - h, PX, plane, 0)
            totals += lax.fori_loop(PX, PX + half, inside, (zero, zero))
            if h > 0:
                lax.fori_loop(PX + half, PX + half + h, plane, 0)
        return totals

    def position(axes):
        flat = 0
        for a in axes:
            flat = flat * lax.axis_size(a) + lax.axis_index(a)
        return flat

    def reduce_all(accs, turn):
        n = len(accs)
        size = -(-n // 8) * 8
        eye = lax.broadcasted_iota(jnp.int32, (size, LANES), 0) == lax.broadcasted_iota(jnp.int32, (size, LANES), 1)
        tall = jnp.concatenate([jnp.sum(a, axis=0, keepdims=True) for a in accs]
                               + [jnp.zeros((size - n, LANES), jnp.float32)] * (size > n), axis=0)
        col = jnp.sum(tall, axis=1, keepdims=True)
        line = jnp.sum(jnp.where(eye, col, 0.0), axis=0, keepdims=True)
        for s, axes in enumerate(stages):
            count = 1
            for a in axes:
                count *= lax.axis_size(a)
            me = position(axes)
            cell = slots[s].at[turn, pl.ds(me, 1), :]
            cell[...] = line
            copies = []
            for off in range(1, count):
                peer = lax.rem(me + off, count)
                ids = {}
                for a in reversed(axes):
                    ids[a] = lax.rem(peer, lax.axis_size(a))
                    peer = lax.div(peer, lax.axis_size(a))
                copy = pltpu.make_async_remote_copy(
                    src_ref=cell, dst_ref=cell, send_sem=red_send[s].at[turn, off - 1],
                    recv_sem=red_recv[s].at[turn, off - 1], device_id=ids, device_id_type=MESH)
                copy.start()
                copies.append(copy)
            for copy in copies:
                copy.wait_recv()
            line = jnp.sum(slots[s][turn], axis=0, keepdims=True)
            for copy in copies:
                copy.wait_send()
        col = jnp.sum(jnp.where(eye, line, 0.0), axis=1, keepdims=True)
        wide = jnp.broadcast_to(col, (size, LANES))
        return [wide[k:k + 1, :] for k in range(n)]

    own = pl.ds(PY, rows)
    for copy in loads[:2 * parts]:
        copy.wait()
    send_halo(p0, 1, 0)
    send_halo(dmp, ITERS - 1, 1)
    for copy in loads[2 * parts:]:
        copy.wait()
    wait_halo(p0, 1, 0)

    def start_plane(x, carry):
        t, centre = stencil(p0, x, PY, rows)
        for z in range(parts):
            r = src[x - PX, z] - (t[z] + (MID - 1.0) * centre[z])
            heads_p[0, x, z, own, :] = r
            base[x - PX, z] = r
        return carry

    lax.fori_loop(PX, PX + half, start_plane, 0)

    pending = [(p0, 1, 0), (dmp, ITERS - 1, 1)]
    slot = 2
    for turn in range(STEPS + 1):
        with_p, with_c = turn < STEPS, turn > 0
        fields = []
        if with_p:
            fields.append((heads_p.at[turn], work_p))
        if with_c:
            fields.append((heads_c.at[turn - 1], work_c))
        slots_here = []
        for head, _ in fields:
            send_halo(head, ITERS, slot)
            slots_here.append((head, ITERS, slot))
            slot += 1
        if turn == 0:
            wait_halo(dmp, ITERS - 1, 1)
        accs = []
        for (head, work), item in zip(fields, slots_here):
            wait_halo(*item)
            accs += powers(head, work)
        pending += slots_here
        dots = reduce_all(accs, turn)
        coeff = [cg_coefficients(dots[6 * i:6 * i + 6]) for i in range(len(fields))]

        def update(i, carry, turn=turn, with_p=with_p, with_c=with_c, fields=fields, coeff=coeff):
            x = i + PX

            def basis(f, z):
                head, work = fields[f]
                return [head[x, z, own, :]] + [work[k, x, z, own, :] for k in range(ITERS)]

            def combine(c, v):
                total = c[0] * v[0]
                for a, b in zip(c[1:], v[1:]):
                    total = total + a * b
                return total

            for z in range(parts):
                line = base[i, z] if turn < STEPS else None
                if with_p:
                    v = basis(0, z)
                    rise = combine(coeff[0][0], v)
                    change = combine(coeff[0][1], v)
                    before = p0[x, z, own, :] if turn == 0 else sums[0, i, z]
                    if turn + 1 < STEPS:
                        sums[0, i, z] = before + rise
                        heads_p[turn + 1, x, z, own, :] = v[0] - change
                    else:
                        result[0, i, z] = before + rise
                if with_c:
                    v = basis(len(fields) - 1, z)
                    rise = combine(coeff[-1][0], v)
                    before = p0[x, z, own, :] if turn == 1 else sums[1, i, z]
                    if turn < STEPS:
                        sums[1, i, z] = before + rise
                        line = line - combine(coeff[-1][1], v)
                        base[i, z] = line
                    else:
                        result[1, i, z] = before + rise
                if turn < STEPS:
                    heads_c[turn, x, z, own, :] = line + 0.5 * change
            return carry

        lax.fori_loop(0, half, update, 0)

    ends = []
    for other in range(1, levels):
        to = lax.rem(level + other, levels)
        for z in range(parts):
            lanes = slice(z * LANES, (z + 1) * LANES)
            copy = pltpu.make_async_remote_copy(
                src_ref=result.at[to, :, z, :, :], dst_ref=out_ref.at[0, mine, :, lanes],
                send_sem=out_sem.at[0, z], recv_sem=out_sem.at[1, z],
                device_id={"level": to, "gx": gx, "yz": yz}, device_id_type=MESH)
            copy.start()
            ends.append(copy)
    for z in range(parts):
        lanes = slice(z * LANES, (z + 1) * LANES)
        copy = pltpu.make_async_copy(result.at[level, :, z, :, :], out_ref.at[0, mine, :, lanes], out_sem.at[2, z])
        copy.start()
        ends.append(copy)
    for item in pending:
        end_halo(*item)
    for copy in ends:
        copy.wait()


def solution(mesh):
    levels, nx, ny = mesh.shape["level"], mesh.shape["gx"], mesh.shape["yz"]
    if levels * nx * ny <= 64:
        stages = (("level", "gx", "yz"),)
    else:
        stages = (("level", "gx"), ("yz",))

    def per_device(init_field, source, damping):
        deep, rows, wide = init_field.shape
        half, parts = deep // levels, wide // LANES
        padded = (half + 2 * PX, parts, rows + 2 * PY, LANES)
        plain = (half, parts, rows, LANES)
        counts = []
        for axes in stages:
            n = 1
            for a in axes:
                n *= mesh.shape[a]
            counts.append(n)
        turns = STEPS + 1
        dma = pltpu.SemaphoreType.DMA
        exchanges = 2 + 2 * STEPS
        return pl.pallas_call(
            functools.partial(body, (levels, nx, ny), stages),
            out_shape=jax.ShapeDtypeStruct((1, deep, rows, wide), jnp.float32),
            in_specs=[pl.BlockSpec(memory_space=pl.ANY)] * 3,
            out_specs=pl.BlockSpec(memory_space=pl.ANY),
            scratch_shapes=[
                pltpu.VMEM(padded, jnp.float32),
                pltpu.VMEM(plain, jnp.float32),
                pltpu.VMEM(padded, jnp.float32),
                pltpu.VMEM((STEPS,) + padded, jnp.float32),
                pltpu.VMEM((STEPS,) + padded, jnp.float32),
                pltpu.VMEM((ITERS,) + padded, jnp.float32),
                pltpu.VMEM((ITERS,) + padded, jnp.float32),
                pltpu.VMEM(plain, jnp.float32),
                pltpu.VMEM((2,) + plain, jnp.float32),
                pltpu.VMEM((2,) + plain, jnp.float32),
                [pltpu.VMEM((turns, n, LANES), jnp.float32) for n in counts],
                dma((3, parts)),
                dma((exchanges, 8)),
                dma((exchanges, 8)),
                [dma((turns, n - 1)) for n in counts],
                [dma((turns, n - 1)) for n in counts],
                dma((3, parts)),
            ],
            compiler_params=pltpu.CompilerParams(has_side_effects=True),
        )(init_field, source, damping)

    spec = P("gx", "yz", None)
    return jax.shard_map(
        per_device, mesh=mesh, in_specs=(spec, spec, spec),
        out_specs=P("level", "gx", "yz", None), check_vma=False,
    )
```

time: 861 us -> 83.6 us (0.10)
  blocking collectives: 477 us -> 0 us
  starting transfers between devices: 204 us -> 0 us
  waiting for transfers between devices: 103 us -> 0 us
  Pallas kernels: 0 us -> 81.6 us
  between operations: 39.6 us -> 0.01 us
  other arithmetic: 27.4 us -> 0 us
    psum x12 -> x0, blocking collectives: 477 us -> none  [two_products(): lax.psum((jnp.sum(resid * resid), jnp.sum(resid * image)), ('gx', 'yz'))]
    ppermute x79 -> x0, starting transfers between devices: 204 us -> none  [the longest x38 150 us: extended(): lax.ppermute(tail, axis, [(i, (i + 1) % count) for i in range(ends)])]
    ppermute x79 -> x0, waiting for transfers between devices: 103 us -> none  [the longest x38 79.6 us: extended(): lax.ppermute(head, axis, [((i + 1) % count, i) for i in range(ends)])]
    pallas_call x0 -> x1, Pallas kernels: none -> 81.6 us  [per_device(): pl.pallas_call(functools.partial(body, (levels, nx, ny), stages), out_sha...]
    reduce_sum x12 -> x0, other arithmetic: 16.3 us -> none  [two_products(): jnp.sum(resid * image)]
  transfers between devices with their start and end apart: 79 -> 0, of which waited for: 42 -> 0; matrix products, arithmetic and copies ran while one was open for 1% -> 0% of each run, Pallas kernels for 0% -> 0%
where the time goes in v1:
time: 83.6 us; the launch traced here: 83.4 us
  Pallas kernels  81.6 us (98%)
  local copies, waits for them, and re-layouts  1.87 us (2%)
    pallas_call x1, Pallas kernels, per_device(): pl.pallas_call(functools.partial(body, (levels, nx, ny), stages), out_sha...  81.6 us
    unnamed x1, local copies, waits for them, and re-layouts  1.87 us

profile of v1, /device:TPU:0, one launch (start us, length us, event | category | flops | bytes accessed | tf_op | source)
XLA Modules:
  0.0 83.4 jit_solution(6144821003209780150)
XLA Ops:
  0.0 81.6 %shard_map.37 = f32[1,32,16,256]{3,2,1,0:T(8,128)} custom-call(f32[32,16,256]{2,1,0:T(8,128)} %init_ref.1, f32[32,16,256]{2,1,0:T(8,128)} %source_ref.1, f32[32,16,256]{2,1,0:T(8,128)} %damp_ref.1), custom_call_target="tpu_custom_call" | custom-call | tf_op jit(solution)/shard_map/pallas_call | solution.py:408
  81.6 1.9 %copy.5 = f32[1,32,16,256]{3,2,1,0:T(8,128)} copy(f32[1,32,16,256]{3,2,1,0:T(8,128)} %shard_map.37) | data formatting | bytes 1048576

commit v2 on v1

--- a/solution.py
+++ b/solution.py
@@ -186,8 +186,6 @@
 
     low = jnp.where(y_in[0], 0, PY)
     high = jnp.where(y_in[1], 2 * PY + rows, PY + rows)
-    first = jnp.where(x_in[0], 0, PX)
-    last = jnp.where(x_in[1], 2 * PX + half, PX + half)
 
     def fold(block):
         return jnp.sum(block.reshape(-1, 8, LANES), axis=0)
@@ -203,37 +201,36 @@
             prev = head if k == 1 else work.at[k - 2]
             row = lax.broadcasted_iota(jnp.int32, (count, LANES), 0) + start
 
-            def plane(x, carry, k=k, h=h, start=start, count=count, prev=prev, row=row):
+            mask = jnp.logical_and(row >= low, row < high)
+            keep = jnp.logical_and(row >= PY, row < PY + rows)
+            older = None if k == 1 else head if k == 2 else work.at[k - 3]
+
+            def plane(x, inner, sides, k=k, h=h, start=start, count=count, prev=prev, mask=mask, keep=keep, older=older):
+                a, b = sides
                 t, centre = stencil(prev, x, start, count)
-                if h > 0:
-                    top = jnp.where(jnp.logical_and(x >= first, x < last), high, 0)
-                    ok = jnp.logical_and(row >= low, row < top)
+                ok = mask
+                if not inner:
+                    ok = jnp.logical_and(mask, x_in[0] if x < PX else x_in[1])
                 for z in range(parts):
                     if k == 1:
                         new = t[z] * (1.0 / HALF)
                     else:
-                        older = head if k == 2 else work.at[k - 3]
                         new = t[z] * (2.0 / HALF) - older[x, z, pl.ds(start, count), :]
                     if h > 0:
                         new = jnp.where(ok, new, 0.0)
                     work[k - 1, x, z, pl.ds(start, count), :] = new
-                return carry
-
-            def inside(x, carry, k=k, prev=prev, plane=plane):
-                plane(x, 0)
-                a, b = carry
-                for z in range(parts):
-                    v = prev[x, z, own, :]
-                    w = work[k - 1, x, z, own, :]
-                    a = a + fold(v * v)
-                    b = b + fold(v * w)
+                    if inner:
+                        square, cross = centre[z] * centre[z], centre[z] * new
+                        if h > 0:
+                            square, cross = jnp.where(keep, square, 0.0), jnp.where(keep, cross, 0.0)
+                        a = a + fold(square)
+                        b = b + fold(cross)
                 return a, b
 
-            if h > 0:
-                lax.fori_loop(PX - h, PX, plane, 0)
-            totals += lax.fori_loop(PX, PX + half, inside, (zero, zero))
-            if h > 0:
-                lax.fori_loop(PX + half, PX + half + h, plane, 0)
+            sides = (zero, zero)
+            for x in range(PX - h, PX + half + h):
+                sides = plane(x, PX <= x < PX + half, sides)
+            totals += sides
         return totals
 
     def position(axes):

time: 83.6 us -> 57.9 us (0.69)
  Pallas kernels: 81.6 us -> 55.8 us
    pallas_call x1, Pallas kernels: 81.6 us -> 55.8 us  [per_device(): pl.pallas_call(functools.partial(body, (levels, nx, ny), stages), out_sha...]
where the time goes in v2:
time: 57.9 us; the launch traced here: 57.7 us
  Pallas kernels  55.8 us (96%)
  local copies, waits for them, and re-layouts  1.87 us (3%)
    pallas_call x1, Pallas kernels, per_device(): pl.pallas_call(functools.partial(body, (levels, nx, ny), stages), out_sha...  55.8 us
    unnamed x1, local copies, waits for them, and re-layouts  1.87 us

profile of v2, /device:TPU:0, one launch (start us, length us, event | category | flops | bytes accessed | tf_op | source)
XLA Modules:
  0.0 57.7 jit_solution(5171399322502611000)
XLA Ops:
  0.0 55.8 %shard_map.37 = f32[1,32,16,256]{3,2,1,0:T(8,128)} custom-call(f32[32,16,256]{2,1,0:T(8,128)} %init_ref.1, f32[32,16,256]{2,1,0:T(8,128)} %source_ref.1, f32[32,16,256]{2,1,0:T(8,128)} %damp_ref.1), custom_call_target="tpu_custom_call" | custom-call | tf_op jit(solution)/shard_map/pallas_call | solution.py:405
  55.9 1.9 %copy.5 = f32[1,32,16,256]{3,2,1,0:T(8,128)} copy(f32[1,32,16,256]{3,2,1,0:T(8,128)} %shard_map.37) | data formatting | bytes 1048576

commit v3 on v2

--- a/solution.py
+++ b/solution.py
@@ -76,7 +76,7 @@
 
 
 def body(sizes, stages, init_ref, source_ref, damp_ref, out_ref, p0, src, dmp, heads_p, heads_c,
-         work_p, work_c, base, sums, result, slots, in_sem, send_sem, recv_sem, red_send, red_recv, out_sem):
+         work_p, work_c, ahead, base, sums, result, inbox, slots, in_sem, send_sem, recv_sem, red_send, red_recv, out_sem):
     levels, nx, ny = sizes
     half = src.shape[0]
     parts = src.shape[1]
@@ -124,7 +124,7 @@
         def _(buf=buf):
             buf[:, :, PY + rows:, :] = zero_y
 
-    def halo_copy(buf, width, slot, k):
+    def halo_copy(buf, width, slot, k, into=None):
         dx, dy = DIRS[k]
         w = width if 0 in (dx, dy) else width - 1
         if w == 0:
@@ -141,7 +141,7 @@
         sy, ty = spans(dy, PY, rows)
         to = xpos + dx
         return pltpu.make_async_remote_copy(
-            src_ref=buf.at[sx, :, sy, :], dst_ref=buf.at[tx, :, ty, :],
+            src_ref=buf.at[sx, :, sy, :], dst_ref=(buf if into is None else into).at[tx, :, ty, :],
             send_sem=send_sem.at[slot, k], recv_sem=recv_sem.at[slot, k],
             device_id={"level": lax.rem(to + levels, levels), "gx": lax.div(to + levels, levels) - 1, "yz": yz + dy},
             device_id_type=MESH,
@@ -149,22 +149,22 @@
 
     order = (4, 5, 6, 7, 2, 3, 0, 1)
 
-    def send_halo(buf, width, slot):
+    def send_halo(buf, width, slot, into=None):
         for k in order:
-            copy = halo_copy(buf, width, slot, k)
+            copy = halo_copy(buf, width, slot, k, into)
             if copy is not None:
                 pl.when(exists(*DIRS[k]))(lambda copy=copy: copy.start())
 
-    def wait_halo(buf, width, slot):
+    def wait_halo(buf, width, slot, into=None):
         for k in order:
-            copy = halo_copy(buf, width, slot, k)
+            copy = halo_copy(buf, width, slot, k, into)
             if copy is not None:
                 dx, dy = DIRS[k]
                 pl.when(exists(-dx, -dy))(lambda copy=copy: copy.wait_recv())
 
-    def end_halo(buf, width, slot):
+    def end_halo(buf, width, slot, into=None):
         for k in order:
-            copy = halo_copy(buf, width, slot, k)
+            copy = halo_copy(buf, width, slot, k, into)
             if copy is not None:
                 pl.when(exists(*DIRS[k]))(lambda copy=copy: copy.wait_send())
 
@@ -239,7 +239,7 @@
             flat = flat * lax.axis_size(a) + lax.axis_index(a)
         return flat
 
-    def reduce_all(accs, turn):
+    def reduce_all(accs, turn, meanwhile):
         n = len(accs)
         size = -(-n // 8) * 8
         eye = lax.broadcasted_iota(jnp.int32, (size, LANES), 0) == lax.broadcasted_iota(jnp.int32, (size, LANES), 1)
@@ -266,6 +266,9 @@
                     recv_sem=red_recv[s].at[turn, off - 1], device_id=ids, device_id_type=MESH)
                 copy.start()
                 copies.append(copy)
+            if s == 0:
+                for item in meanwhile:
+                    send_halo(*item)
             for copy in copies:
                 copy.wait_recv()
             line = jnp.sum(slots[s][turn], axis=0, keepdims=True)
@@ -275,6 +278,24 @@
         wide = jnp.broadcast_to(col, (size, LANES))
         return [wide[k:k + 1, :] for k in range(n)]
 
+    def to_out(block, part, row):
+        return [pltpu.make_async_copy(
+            block.at[:, z, :, :], out_ref.at[0, pl.ds(part * half, half), :, slice(z * LANES, (z + 1) * LANES)],
+            out_sem.at[row, z]) for z in range(parts)]
+
+    def pieces(f):
+        return to_out(result.at[f], level, 2)
+
+    def across(f):
+        return pltpu.make_async_remote_copy(
+            src_ref=result.at[f], dst_ref=inbox, send_sem=out_sem.at[0, 0], recv_sem=out_sem.at[1, 0],
+            device_id={"level": f, "gx": gx, "yz": yz}, device_id_type=MESH)
+
+    def deliver(f):
+        pl.when(level != f)(lambda: across(f).start())
+        for copy in pieces(f):
+            pl.when(level == f)(lambda copy=copy: copy.start())
+
     own = pl.ds(PY, rows)
     for copy in loads[:2 * parts]:
         copy.wait()
@@ -292,7 +313,7 @@
             base[x - PX, z] = r
         return carry
 
-    lax.fori_loop(PX, PX + half, start_plane, 0)
+    lax.fori_loop(PX, PX + half, start_plane, 0, unroll=True)
 
     pending = [(p0, 1, 0), (dmp, ITERS - 1, 1)]
     slot = 2
@@ -305,17 +326,25 @@
             fields.append((heads_c.at[turn - 1], work_c))
         slots_here = []
         for head, _ in fields:
-            send_halo(head, ITERS, slot)
-            slots_here.append((head, ITERS, slot))
-            slot += 1
+            if turn != 1:
+                send_halo(head, ITERS, slot)
+                slots_here.append((head, ITERS, slot))
+                slot += 1
         if turn == 0:
             wait_halo(dmp, ITERS - 1, 1)
         accs = []
-        for (head, work), item in zip(fields, slots_here):
-            wait_halo(*item)
+        for i, (head, work) in enumerate(fields):
+            if turn != 1:
+                wait_halo(*slots_here[i])
             accs += powers(head, work)
         pending += slots_here
-        dots = reduce_all(accs, turn)
+        outer = []
+        if turn == 0:
+            for k in range(ITERS):
+                outer.append((work_p.at[k], ITERS, slot, ahead.at[k]))
+                slot += 1
+            pending += outer
+        dots = reduce_all(accs, turn, outer)
         coeff = [cg_coefficients(dots[6 * i:6 * i + 6]) for i in range(len(fields))]
 
         def update(i, carry, turn=turn, with_p=with_p, with_c=with_c, fields=fields, coeff=coeff):
@@ -357,26 +386,47 @@
                     heads_c[turn, x, z, own, :] = line + 0.5 * change
             return carry
 
-        lax.fori_loop(0, half, update, 0)
-
-    ends = []
-    for other in range(1, levels):
-        to = lax.rem(level + other, levels)
-        for z in range(parts):
-            lanes = slice(z * LANES, (z + 1) * LANES)
-            copy = pltpu.make_async_remote_copy(
-                src_ref=result.at[to, :, z, :, :], dst_ref=out_ref.at[0, mine, :, lanes],
-                send_sem=out_sem.at[0, z], recv_sem=out_sem.at[1, z],
-                device_id={"level": to, "gx": gx, "yz": yz}, device_id_type=MESH)
-            copy.start()
-            ends.append(copy)
-    for z in range(parts):
-        lanes = slice(z * LANES, (z + 1) * LANES)
-        copy = pltpu.make_async_copy(result.at[level, :, z, :, :], out_ref.at[0, mine, :, lanes], out_sem.at[2, z])
-        copy.start()
-        ends.append(copy)
+        lax.fori_loop(0, half, update, 0, unroll=True)
+        if turn == 0:
+            for item in outer:
+                wait_halo(*item)
+                end_halo(*item)
+            pending = pending[:-len(outer)]
+
+            def rim(x, begin, count, plane_ok):
+                span = pl.ds(begin, count)
+                row = lax.broadcasted_iota(jnp.int32, (count, LANES), 0) + begin
+                ok = jnp.logical_and(row >= low, row < high)
+                if plane_ok is not None:
+                    ok = jnp.logical_and(ok, plane_ok)
+                for z in range(parts):
+                    now = heads_p[0, x, z, span, :]
+                    change = coeff[0][1][0] * now
+                    for k in range(ITERS):
+                        change = change + coeff[0][1][k + 1] * ahead[k, x, z, span, :]
+                    heads_p[1, x, z, span, :] = jnp.where(ok, now - change, 0.0)
+                    heads_c[0, x, z, span, :] = jnp.where(ok, now + 0.5 * change, 0.0)
+
+            for x in range(PX):
+                rim(x, 0, 2 * PY + rows, x_in[0])
+                rim(PX + half + x, 0, 2 * PY + rows, x_in[1])
+            for x in range(PX, PX + half):
+                rim(x, 0, PY, None)
+                rim(x, PY + rows, PY, None)
+        if turn == STEPS - 1:
+            deliver(0)
+    deliver(1)
+
     for item in pending:
         end_halo(*item)
+    for f in range(2):
+        pl.when(level != f)(lambda f=f: across(f).wait_send())
+        pl.when(level == f)(lambda f=f: across(f).wait_recv())
+        for copy in pieces(f):
+            pl.when(level == f)(lambda copy=copy: copy.wait())
+    ends = to_out(inbox, 1 - level, 3)
+    for copy in ends:
+        copy.start()
     for copy in ends:
         copy.wait()
 
@@ -401,7 +451,7 @@
             counts.append(n)
         turns = STEPS + 1
         dma = pltpu.SemaphoreType.DMA
-        exchanges = 2 + 2 * STEPS
+        exchanges = 2 + 2 * STEPS + ITERS
         return pl.pallas_call(
             functools.partial(body, (levels, nx, ny), stages),
             out_shape=jax.ShapeDtypeStruct((1, deep, rows, wide), jnp.float32),
@@ -415,16 +465,18 @@
                 pltpu.VMEM((STEPS,) + padded, jnp.float32),
                 pltpu.VMEM((ITERS,) + padded, jnp.float32),
                 pltpu.VMEM((ITERS,) + padded, jnp.float32),
+                pltpu.VMEM((ITERS,) + padded, jnp.float32),
                 pltpu.VMEM(plain, jnp.float32),
                 pltpu.VMEM((2,) + plain, jnp.float32),
                 pltpu.VMEM((2,) + plain, jnp.float32),
+                pltpu.VMEM(plain, jnp.float32),
                 [pltpu.VMEM((turns, n, LANES), jnp.float32) for n in counts],
                 dma((3, parts)),
                 dma((exchanges, 8)),
                 dma((exchanges, 8)),
                 [dma((turns, n - 1)) for n in counts],
                 [dma((turns, n - 1)) for n in counts],
-                dma((3, parts)),
+                dma((4, parts)),
             ],
             compiler_params=pltpu.CompilerParams(has_side_effects=True),
         )(init_field, source, damping)

time: 57.9 us -> 56.2 us (0.971)
  Pallas kernels: 55.8 us -> 54.2 us
    pallas_call x1, Pallas kernels: 55.8 us -> 54.2 us  [per_device(): pl.pallas_call(functools.partial(body, (levels, nx, ny), stages), out_sha...]
where the time goes in v3:
time: 56.2 us; the launch traced here: 56 us
  Pallas kernels  54.2 us (96%)
  local copies, waits for them, and re-layouts  1.87 us (3%)
    pallas_call x1, Pallas kernels, per_device(): pl.pallas_call(functools.partial(body, (levels, nx, ny), stages), out_sha...  54.2 us
    unnamed x1, local copies, waits for them, and re-layouts  1.87 us

profile of v3, /device:TPU:0, one launch (start us, length us, event | category | flops | bytes accessed | tf_op | source)
XLA Modules:
  0.0 56.0 jit_solution(17339958370627739105)
XLA Ops:
  0.0 54.2 %shard_map.37 = f32[1,32,16,256]{3,2,1,0:T(8,128)} custom-call(f32[32,16,256]{2,1,0:T(8,128)} %init_ref.1, f32[32,16,256]{2,1,0:T(8,128)} %source_ref.1, f32[32,16,256]{2,1,0:T(8,128)} %damp_ref.1), custom_call_target="tpu_custom_call" | custom-call | tf_op jit(solution)/shard_map/pallas_call | solution.py:455
  54.2 1.9 %copy.5 = f32[1,32,16,256]{3,2,1,0:T(8,128)} copy(f32[1,32,16,256]{3,2,1,0:T(8,128)} %shard_map.37) | data formatting | bytes 1048576
